TPU v7x, 128 devices: a whole 4x4x4 slice. The times are simulated.
128 devices in a mesh: expert: 4 (over x_lo, core), shard: 32 (over z, y, x_hi).
Axes of the slice: x: 4 (x_hi: 2, x_lo: 2; x = x_hi * 2 + x_lo), y: 4, z: 4, core: 2. Of those that a mesh axis runs over, the one named last changes fastest.
Arguments:
- master_gate: float32 [64, 2048, 1024], P('expert', 'shard'), may hold values from -0.25 to 0.25
- second_gate: bfloat16 [64, 2048, 1024], P('expert', 'shard'), may hold values from -0.0625 to 0.0625
- master_up: float32 [64, 2048, 1024], P('expert', 'shard'), may hold values from -0.25 to 0.25
- second_up: bfloat16 [64, 2048, 1024], P('expert', 'shard'), may hold values from -0.0625 to 0.0625
- master_down: float32 [64, 1024, 2048], P('expert', None, 'shard'), may hold values from -0.375 to 0.375
- second_down: bfloat16 [64, 1024, 2048], P('expert', None, 'shard'), may hold values from -0.09375 to 0.09375
- router_weight: float32 [2048, 64], P('shard', 'expert'), may hold values from -0.125 to 0.125
- router_gain: float32 [2048], P('shard'), may hold values from 0.25 to 1.75
Outputs:
- final_gate: bfloat16 [64, 2048, 1024], P('expert', None, 'shard')
- final_up: bfloat16 [64, 2048, 1024], P('expert', None, 'shard')
- final_down: bfloat16 [64, 1024, 2048], P('expert', 'shard')
- scale_gate: float32 [64, 1024], P('expert', 'shard')
- scale_up: float32 [64, 1024], P('expert', 'shard')
- scale_down: float32 [64, 1024], P('expert', 'shard')
- serve_router: bfloat16 [2048, 64], replicated
All inputs are finite; a program needn't handle non-finite values. Where the computation divides by a largest or mean magnitude, that divisor is 1e-20 or more.
Results may differ from a plain program's by a relative error of at most 0.001.
Values may be sent and summed in bfloat16 or wider, within the bound.
A program may use at most 128 MiB of HBM per device.

v0:
```python
import jax
import jax.numpy as jnp
from jax import lax
from jax.sharding import PartitionSpec as P


def over_pieces(array, axis):
    blocks = lax.all_gather(array, axis)
    return blocks.max(axis=0)


def joined_along(blocks, dim):
    blocks = jnp.moveaxis(blocks, 0, dim)
    lengths = blocks.shape
    return blocks.reshape(*lengths[:dim], lengths[dim] * lengths[dim + 1], *lengths[dim + 2 :])


def copy_for_each(array, axis):
    copies = jnp.broadcast_to(array, (lax.axis_size(axis), *array.shape))
    return lax.all_to_all(copies, axis, split_axis=0, concat_axis=0, tiled=True)


def gather_directly(array, axis, dim):
    return joined_along(copy_for_each(array, axis), dim)


def per_device(
    master_gate,
    second_gate,
    master_up,
    second_up,
    master_down,
    second_down,
    router_weight,
    router_gain,
):
    merged_gate = master_gate + second_gate.astype(jnp.float32)
    merged_up = master_up + second_up.astype(jnp.float32)
    merged_down = master_down + second_down.astype(jnp.float32)
    scale_gate, scale_up, scale_down = (
        over_pieces(jnp.max(jnp.abs(merged_gate), axis=1), "shard"),
        over_pieces(jnp.max(jnp.abs(merged_up), axis=1), "shard"),
        over_pieces(jnp.max(jnp.abs(merged_down), axis=2), "shard"),
    )
    narrow_gate, narrow_up, narrow_down = (
        (merged_gate / jnp.expand_dims(scale_gate, 1)).astype(jnp.bfloat16),
        (merged_up / jnp.expand_dims(scale_up, 1)).astype(jnp.bfloat16),
        (merged_down / jnp.expand_dims(scale_down, 2)).astype(jnp.bfloat16),
    )
    final_gate, final_up = (
        lax.all_to_all(narrow_gate, "shard", split_axis=2, concat_axis=1, tiled=True),
        lax.all_to_all(narrow_up, "shard", split_axis=2, concat_axis=1, tiled=True),
    )
    final_down = lax.all_to_all(narrow_down, "shard", split_axis=1, concat_axis=2, tiled=True)
    scale_gate = lax.dynamic_slice_in_dim(
        scale_gate, lax.axis_index("shard") * final_gate.shape[2], final_gate.shape[2], axis=1
    )
    scale_up = lax.dynamic_slice_in_dim(
        scale_up, lax.axis_index("shard") * final_up.shape[2], final_up.shape[2], axis=1
    )
    scale_down = lax.dynamic_slice_in_dim(
        scale_down, lax.axis_index("shard") * final_down.shape[1], final_down.shape[1], axis=1
    )
    part_router = (router_weight * router_gain[:, None]).astype(jnp.bfloat16)
    row_router = gather_directly(part_router, "shard", 0)
    serve_router = gather_directly(row_router, "expert", 1)
    return (final_gate, final_up, final_down, scale_gate, scale_up, scale_down, serve_router)


def solution(mesh):
    in_specs = (
        P("expert", "shard", None),
        P("expert", "shard", None),
        P("expert", "shard", None),
        P("expert", "shard", None),
        P("expert", None, "shard"),
        P("expert", None, "shard"),
        P("shard", "expert"),
        P("shard"),
    )
    out_specs = (
        P("expert", None, "shard"),
        P("expert", None, "shard"),
        P("expert", "shard", None),
        P("expert", "shard"),
        P("expert", "shard"),
        P("expert", "shard"),
        P(),
    )
    return jax.shard_map(
        per_device, mesh=mesh, in_specs=in_specs, out_specs=out_specs, check_vma=False
    )
```

profile of v0, /device:TPU:6, one launch (start us, length us, event | category | flops | bytes accessed | tf_op | source)
XLA Modules:
  0.0 352.2 jit_solution(11286700278686036596)
XLA Ops:
  7.2 0.0 copy-start.1
  7.2 0.0 all-gather.7.cloned.1.call-start
  7.2 4.4 %abs_reduce_fusion.2 = f32[16,1024]{1,0:T(8,128)} fusion(f32[16,64,1024]{2,1,0:T(8,128)} %param.8, bf16[16,64,1024]{2,1,0:T(8,128)(2,1)} %param.9), kind=kLoop, calls=%fused_computation.7 | loop fusion | flops 4177920 | bytes 6356992 | tf_op jit(solution)/shard_map/reduce_max | solution.py:41
  11.6 0.0 all-gather.7.cloned.1.call-update
  11.7 0.0 all-gather.9.cloned.1.call-start
  11.7 3.6 %abs_reduce_fusion.1 = f32[16,1024]{1,0:T(8,128)} fusion(f32[16,64,1024]{2,1,0:T(8,128)} %param.10, bf16[16,64,1024]{2,1,0:T(8,128)(2,1)S(1)} %copy-done.1), kind=kLoop, calls=%fused_computation.4 | loop fusion | flops 4177920 | bytes 6356992 | tf_op jit(solution)/shard_map/reduce_max | solution.py:42
  15.3 0.0 all-gather.9.cloned.1.call-update
  15.4 0.8 reshape.35
  16.2 11.1 %all-to-all-start.3 = ((bf16[32,2,512]{2,1,0:T(2,128)(2,1)}), bf16[32,2,512]{2,1,0:T(2,128)(2,1)S(1)}, u32[]{:S(2)}, u32[]{:S(2)}) async-start(bf16[32,2,512]{2,1,0:T(2,128)(2,1)} %reshape.35), calls=%async_computation.3 | async-start | bytes 131072 | tf_op jit(solution)/shard_map/all_to_all | solution.py:20
  27.2 0.0 all-gather.11.cloned.1.call-start
  27.3 4.4 %abs_reduce_fusion = f32[16,1024]{1,0:T(8,128)} fusion(f32[16,1024,64]{1,2,0:T(8,128)} %param.12, bf16[16,1024,64]{1,2,0:T(8,128)(2,1)} %param.13), kind=kLoop, calls=%fused_computation.1 | loop fusion | flops 4177920 | bytes 6356992 | tf_op jit(solution)/shard_map/reduce_max | solution.py:43
  31.7 0.0 all-gather.11.cloned.1.call-update
  31.7 2.8 all-to-all-done.3
  34.6 0.1 reshape.36
  34.7 0.2 reshape.24
  34.9 0.7 broadcast_in_dim.5
  35.6 4.2 %all-to-all-start.4 = ((bf16[4,2048,16]{1,2,0:T(8,128)(2,1)}), bf16[4,2048,16]{1,2,0:T(8,128)(2,1)S(1)}, u32[]{:S(2)}, u32[]{:S(2)}) async-start(bf16[4,2048,16]{1,2,0:T(8,128)(2,1)} %broadcast_in_dim.5), calls=%async_computation.4 | async-start | bytes 524288 | tf_op jit(solution)/shard_map/all_to_all | solution.py:20
  39.9 43.3 %all-gather.7.cloned.1.call-done = f32[512,1024]{1,0:T(8,128)} async-done(((f32[16,1024]{1,0:T(8,128)}), f32[512,1024]{1,0:T(8,128)}) %all-gather.7.cloned.1.call-update) | async-done | bytes 2097168 | tf_op jit(solution)/shard_map/all_gather | solution.py:8
  83.1 1.7 reduce_max.55
  84.8 4.4 %divide_convert_fusion.2 = bf16[16,64,1024]{2,1,0:T(8,128)(2,1)} fusion(f32[16,64,1024]{2,1,0:T(8,128)} %param.8, bf16[16,64,1024]{2,1,0:T(8,128)(2,1)S(1)} %copy-done, f32[16,1024]{1,0:T(8,128)S(1)} %reduce_max.55), kind=kLoop, calls=%fused_computation.6 | loop fusion | flops 4194304 | bytes 8454144 | tf_op jit(solution)/shard_map/convert_element_type | solution.py:46
  89.2 6.2 %copy.120 = bf16[16,64,1024]{1,0,2:T(8,128)(2,1)} copy(bf16[16,64,1024]{2,1,0:T(8,128)(2,1)} %divide_convert_fusion.2) | data formatting | bytes 4194304 | tf_op jit(solution)/shard_map/convert_element_type | solution.py:46
  95.4 7.9 %reshape.29 = bf16[32,2,16384]{2,1,0:T(2,128)(2,1)} reshape(bf16[1024,16,64]{2,1,0:T(8,128)(2,1)} %bitcast.36) | data formatting | bytes 4194304
  103.3 8.6 %all-to-all-start = ((bf16[32,2,16384]{2,1,0:T(2,128)(2,1)}), bf16[32,2,16384]{2,1,0:T(2,128)(2,1)S(1)}, u32[]{:S(2)}, u32[]{:S(2)}) async-start(bf16[32,2,16384]{2,1,0:T(2,128)(2,1)} %reshape.29), calls=%async_computation | async-start | bytes 4194304 | tf_op jit(solution)/shard_map/all_to_all | solution.py:51
  111.9 55.8 %all-gather.9.cloned.1.call-done = f32[512,1024]{1,0:T(8,128)} async-done(((f32[16,1024]{1,0:T(8,128)}), f32[512,1024]{1,0:T(8,128)}) %all-gather.9.cloned.1.call-update) | async-done | bytes 2097168 | tf_op jit(solution)/shard_map/all_gather | solution.py:8
  167.7 1.7 reduce_max.57
  169.4 5.0 %divide_convert_fusion.1 = bf16[16,64,1024]{2,1,0:T(8,128)(2,1)} fusion(f32[16,64,1024]{2,1,0:T(8,128)} %param.10, bf16[16,64,1024]{2,1,0:T(8,128)(2,1)} %param.11, f32[16,1024]{1,0:T(8,128)S(1)} %reduce_max.57), kind=kLoop, calls=%fused_computation.3 | loop fusion | flops 4194304 | bytes 8454144 | tf_op jit(solution)/shard_map/convert_element_type | solution.py:47
  174.4 6.2 %copy.125 = bf16[16,64,1024]{1,0,2:T(8,128)(2,1)} copy(bf16[16,64,1024]{2,1,0:T(8,128)(2,1)} %divide_convert_fusion.1) | data formatting | bytes 4194304 | tf_op jit(solution)/shard_map/convert_element_type | solution.py:47
  180.5 7.9 %reshape.31 = bf16[32,2,16384]{2,1,0:T(2,128)(2,1)} reshape(bf16[1024,16,64]{2,1,0:T(8,128)(2,1)} %bitcast.37) | data formatting | bytes 4194304
  188.4 8.6 %all-to-all-start.1 = ((bf16[32,2,16384]{2,1,0:T(2,128)(2,1)}), bf16[32,2,16384]{2,1,0:T(2,128)(2,1)}, u32[]{:S(2)}, u32[]{:S(2)}) async-start(bf16[32,2,16384]{2,1,0:T(2,128)(2,1)} %reshape.31), calls=%async_computation.1 | async-start | bytes 4194304 | tf_op jit(solution)/shard_map/all_to_all | solution.py:52
  197.1 55.7 %all-gather.11.cloned.1.call-done = f32[512,1024]{1,0:T(8,128)} async-done(((f32[16,1024]{1,0:T(8,128)}), f32[512,1024]{1,0:T(8,128)}) %all-gather.11.cloned.1.call-update) | async-done | bytes 2097168 | tf_op jit(solution)/shard_map/all_gather | solution.py:8
  252.8 1.7 reduce_max.59
  254.5 5.0 %divide_convert_fusion = bf16[16,1024,64]{1,2,0:T(8,128)(2,1)} fusion(f32[16,1024,64]{1,2,0:T(8,128)} %param.12, bf16[16,1024,64]{1,2,0:T(8,128)(2,1)} %param.13, f32[16,1024]{1,0:T(8,128)S(1)} %reduce_max.59), kind=kLoop, calls=%fused_computation | loop fusion | flops 4194304 | bytes 8454144 | tf_op jit(solution)/shard_map/convert_element_type | solution.py:48
  259.5 6.2 %copy.130 = bf16[16,1024,64]{2,0,1:T(8,128)(2,1)} copy(bf16[16,1024,64]{1,2,0:T(8,128)(2,1)} %divide_convert_fusion) | data formatting | bytes 4194304 | tf_op jit(solution)/shard_map/convert_element_type | solution.py:48
  265.7 7.9 %reshape.33 = bf16[32,2,16384]{2,1,0:T(2,128)(2,1)} reshape(bf16[1024,16,64]{2,1,0:T(8,128)(2,1)} %bitcast.38) | data formatting | bytes 4194304
  273.6 8.6 %all-to-all-start.2 = ((bf16[32,2,16384]{2,1,0:T(2,128)(2,1)}), bf16[32,2,16384]{2,1,0:T(2,128)(2,1)}, u32[]{:S(2)}, u32[]{:S(2)}) async-start(bf16[32,2,16384]{2,1,0:T(2,128)(2,1)} %reshape.33), calls=%async_computation.2 | async-start | bytes 4194304 | tf_op jit(solution)/shard_map/all_to_all | solution.py:54
  282.2 0.7 constant_dynamic-slice_fusion
  282.9 0.7 constant_dynamic-slice_fusion.1
  283.6 0.7 constant_dynamic-slice_fusion.2
  284.3 4.0 %reshape.30 = bf16[1024,16,64]{2,1,0:T(8,128)(2,1)} reshape(bf16[32,2,16384]{2,1,0:T(2,128)(2,1)S(1)} %all-to-all-done) | data formatting | bytes 4194304
  288.2 6.9 %copy.122 = bf16[16,32,64,32]{2,1,3,0:T(8,128)(2,1)} copy(bf16[16,32,64,32]{2,0,3,1:T(8,128)(2,1)} %bitcast.39) | data formatting | bytes 4194304 | tf_op jit(solution)/shard_map/all_to_all | solution.py:51
  295.1 6.7 %all_to_all.48 = bf16[16,2048,32]{1,2,0:T(8,128)(2,1)} reshape(bf16[16,32,64,32]{2,1,3,0:T(8,128)(2,1)} %copy.122) | data formatting | bytes 4194304 | tf_op jit(solution)/shard_map/all_to_all | solution.py:51
  301.9 7.9 %reshape.32 = bf16[1024,16,64]{2,1,0:T(8,128)(2,1)} reshape(bf16[32,2,16384]{2,1,0:T(2,128)(2,1)} %all-to-all-done.1) | data formatting | bytes 4194304
  309.8 6.9 %copy.127 = bf16[16,32,64,32]{2,1,3,0:T(8,128)(2,1)} copy(bf16[16,32,64,32]{2,0,3,1:T(8,128)(2,1)} %bitcast.40) | data formatting | bytes 4194304 | tf_op jit(solution)/shard_map/all_to_all | solution.py:52
  316.6 6.7 %all_to_all.52 = bf16[16,2048,32]{1,2,0:T(8,128)(2,1)} reshape(bf16[16,32,64,32]{2,1,3,0:T(8,128)(2,1)} %copy.127) | data formatting | bytes 4194304 | tf_op jit(solution)/shard_map/all_to_all | solution.py:52
  323.4 7.9 %reshape.34 = bf16[1024,16,64]{2,1,0:T(8,128)(2,1)} reshape(bf16[32,2,16384]{2,1,0:T(2,128)(2,1)} %all-to-all-done.2) | data formatting | bytes 4194304
  331.3 6.9 %copy.132 = bf16[16,32,32,64]{3,2,1,0:T(8,128)(2,1)} copy(bf16[16,32,32,64]{3,0,1,2:T(8,128)(2,1)} %bitcast.41) | data formatting | bytes 4194304 | tf_op jit(solution)/shard_map/all_to_all | solution.py:54
  338.2 6.7 %all_to_all.56 = bf16[16,32,2048]{2,1,0:T(8,128)(2,1)} reshape(bf16[16,32,32,64]{3,2,1,0:T(8,128)(2,1)} %copy.132) | data formatting | bytes 4194304 | tf_op jit(solution)/shard_map/all_to_all | solution.py:54
  344.9 0.7 copy.141
  (14 shorter events, 0.1 us)
Async XLA Ops:
  7.2 4.5 %copy-start.1 = (bf16[16,64,1024]{2,1,0:T(8,128)(2,1)S(1)}, bf16[16,64,1024]{2,1,0:T(8,128)(2,1)}, u32[]{:S(2)}) copy-start(bf16[16,64,1024]{2,1,0:T(8,128)(2,1)} %param.11) | copy-start | bytes 6291460
  7.2 75.9 %all-gather.7.cloned.1.call-start = ((), (), s32[]{:S(2)}) async-start(), calls=%async_computation.5 | async-start | bytes 2162688 | tf_op jit(solution)/shard_map/all_gather | solution.py:8
  11.6 3.7 %copy-start.2 = (f32[64,16]{0,1:T(8,128)S(1)}, f32[64,16]{0,1:T(8,128)}, u32[]{:S(2)}) copy-start(f32[64,16]{0,1:T(8,128)} %param.14) | copy-start | bytes 12292
  11.6 3.7 %copy-start.3 = (f32[64]{0:T(128)S(1)}, f32[64]{0:T(128)}, u32[]{:S(2)}) copy-start(f32[64]{0:T(128)} %param.15) | copy-start | bytes 772
  11.7 156.0 %all-gather.9.cloned.1.call-start = ((), (), s32[]{:S(2)}) async-start(), calls=%async_computation.6 | async-start | bytes 2162688 | tf_op jit(solution)/shard_map/all_gather | solution.py:8
  16.2 18.4 %all-to-all-start.3 = ((bf16[32,2,512]{2,1,0:T(2,128)(2,1)}), bf16[32,2,512]{2,1,0:T(2,128)(2,1)S(1)}, u32[]{:S(2)}, u32[]{:S(2)}) async-start(bf16[32,2,512]{2,1,0:T(2,128)(2,1)} %reshape.35), calls=%async_computation.3 | async-start | bytes 131072 | tf_op jit(solution)/shard_map/all_to_all | solution.py:20
  27.2 57.6 %copy-start = (bf16[16,64,1024]{2,1,0:T(8,128)(2,1)S(1)}, bf16[16,64,1024]{2,1,0:T(8,128)(2,1)}, u32[]{:S(2)}) copy-start(bf16[16,64,1024]{2,1,0:T(8,128)(2,1)} %param.9) | copy-start | bytes 6291460
  27.2 225.6 %all-gather.11.cloned.1.call-start = ((), (), s32[]{:S(2)}) async-start(), calls=%async_computation.7 | async-start | bytes 2162688 | tf_op jit(solution)/shard_map/all_gather | solution.py:8
  35.6 67.6 %all-to-all-start.4 = ((bf16[4,2048,16]{1,2,0:T(8,128)(2,1)}), bf16[4,2048,16]{1,2,0:T(8,128)(2,1)S(1)}, u32[]{:S(2)}, u32[]{:S(2)}) async-start(bf16[4,2048,16]{1,2,0:T(8,128)(2,1)} %broadcast_in_dim.5), calls=%async_computation.4 | async-start | bytes 524288 | tf_op jit(solution)/shard_map/all_to_all | solution.py:20
  103.3 85.2 %all-to-all-start = ((bf16[32,2,16384]{2,1,0:T(2,128)(2,1)}), bf16[32,2,16384]{2,1,0:T(2,128)(2,1)S(1)}, u32[]{:S(2)}, u32[]{:S(2)}) async-start(bf16[32,2,16384]{2,1,0:T(2,128)(2,1)} %reshape.29), calls=%async_computation | async-start | bytes 4194304 | tf_op jit(solution)/shard_map/all_to_all | solution.py:51
  188.4 85.2 %all-to-all-start.1 = ((bf16[32,2,16384]{2,1,0:T(2,128)(2,1)}), bf16[32,2,16384]{2,1,0:T(2,128)(2,1)}, u32[]{:S(2)}, u32[]{:S(2)}) async-start(bf16[32,2,16384]{2,1,0:T(2,128)(2,1)} %reshape.31), calls=%async_computation.1 | async-start | bytes 4194304 | tf_op jit(solution)/shard_map/all_to_all | solution.py:52
  273.6 49.8 %all-to-all-start.2 = ((bf16[32,2,16384]{2,1,0:T(2,128)(2,1)}), bf16[32,2,16384]{2,1,0:T(2,128)(2,1)}, u32[]{:S(2)}, u32[]{:S(2)}) async-start(bf16[32,2,16384]{2,1,0:T(2,128)(2,1)} %reshape.33), calls=%async_computation.2 | async-start | bytes 4194304 | tf_op jit(solution)/shard_map/all_to_all | solution.py:54
Sparse Core Ops, SparseCore 0:
  11.8 71.2 all-gather.6
  86.8 80.8 all-gather.8
  171.3 81.4 all-gather.10
where the time goes:
time: 354 us; the launch traced here: 352 us
  waiting for transfers between devices  158 us (45%)
  local copies, waits for them, and re-layouts  107 us (30%)
  starting transfers between devices  41.3 us (12%)
  other arithmetic  31.9 us (9%)
  between operations  13.9 us (4%)
    all_gather x3, waiting for transfers between devices, over_pieces(): blocks = lax.all_gather(array, axis)  155 us
    unnamed x18, local copies, waits for them, and re-layouts  45.1 us
    all_to_all x2, starting transfers between devices, copy_for_each(): return lax.all_to_all(copies, axis, split_axis=0, concat_axis=0, tiled=True)  15.3 us
    all_to_all x2, local copies, waits for them, and re-layouts, per_device(): lax.all_to_all(narrow_gate, 'shard', split_axis=2, concat_axis=1, tiled=T...  13.6 us
    all_to_all x2, local copies, waits for them, and re-layouts, per_device(): lax.all_to_all(narrow_down, 'shard', split_axis=1, concat_axis=2, tiled=T...  13.6 us
    all_to_all x2, local copies, waits for them, and re-layouts, per_device(): lax.all_to_all(narrow_up, 'shard', split_axis=2, concat_axis=1, tiled=True)  13.6 us
    all_to_all x1, starting transfers between devices, per_device(): lax.all_to_all(narrow_up, 'shard', split_axis=2, concat_axis=1, tiled=True)  8.64 us
    all_to_all x1, starting transfers between devices, per_device(): lax.all_to_all(narrow_down, 'shard', split_axis=1, concat_axis=2, tiled=T...  8.64 us
  transfers between devices with their start and end apart: 8, of which 4 were waited for; matrix products, arithmetic and copies ran while one was open for 28% of the time, Pallas kernels for 0%

commit v1 on v0

--- a/solution.py
+++ b/solution.py
@@ -48,7 +48,12 @@
         (merged_down / jnp.expand_dims(scale_down, 2)).astype(jnp.bfloat16),
     )
     final_gate, final_up = (
-        lax.all_to_all(narrow_gate, "shard", split_axis=2, concat_axis=1, tiled=True),
+        jnp.concatenate(
+            lax.all_to_all(
+                jnp.stack(jnp.split(narrow_gate, lax.axis_size("shard"), axis=2)), "shard", 0, 0
+            ),
+            axis=1,
+        ),
         lax.all_to_all(narrow_up, "shard", split_axis=2, concat_axis=1, tiled=True),
     )
     final_down = lax.all_to_all(narrow_down, "shard", split_axis=1, concat_axis=2, tiled=True)

time: 354 us -> 367 us (1.037)
  local copies, waits for them, and re-layouts: 107 us -> 115 us
  other arithmetic: 31.9 us -> 36.7 us
    reshape x0 -> x3, local copies, waits for them, and re-layouts: none -> 14.4 us  [per_device(): jnp.concatenate(lax.all_to_all(jnp.stack(jnp.split(narrow_gate, lax.axis_...]
    all_to_all x2 -> x0, local copies, waits for them, and re-layouts: 13.6 us -> none  [per_device(): lax.all_to_all(narrow_gate, 'shard', split_axis=2, concat_axis=1, tiled=T...]
    unnamed x18 -> x53, local copies, waits for them, and re-layouts: 45.1 us -> 57.9 us
    convert_element_type x1 -> x0, local copies, waits for them, and re-layouts: 6.17 us -> none  [per_device(): (merged_gate / jnp.expand_dims(scale_gate, 1)).astype(jnp.bfloat16)]
where the time goes in v1:
time: 367 us; the launch traced here: 365 us
  waiting for transfers between devices  158 us (43%)
  local copies, waits for them, and re-layouts  115 us (31%)
  starting transfers between devices  41.3 us (11%)
  other arithmetic  36.7 us (10%)
  between operations  14.1 us (4%)
    all_gather x3, waiting for transfers between devices, over_pieces(): blocks = lax.all_gather(array, axis)  155 us
    unnamed x53, local copies, waits for them, and re-layouts  57.9 us
    all_to_all x2, starting transfers between devices, copy_for_each(): return lax.all_to_all(copies, axis, split_axis=0, concat_axis=0, tiled=True)  15.3 us
    reshape x3, local copies, waits for them, and re-layouts, per_device(): jnp.concatenate(lax.all_to_all(jnp.stack(jnp.split(narrow_gate, lax.axis_...  14.4 us
    all_to_all x2, local copies, waits for them, and re-layouts, per_device(): lax.all_to_all(narrow_up, 'shard', split_axis=2, concat_axis=1, tiled=True)  13.6 us
    all_to_all x2, local copies, waits for them, and re-layouts, per_device(): lax.all_to_all(narrow_down, 'shard', split_axis=1, concat_axis=2, tiled=T...  13.6 us
    all_to_all x1, starting transfers between devices, per_device(): lax.all_to_all(narrow_down, 'shard', split_axis=1, concat_axis=2, tiled=T...  8.65 us
    all_to_all x1, starting transfers between devices, per_device(): lax.all_to_all(narrow_up, 'shard', split_axis=2, concat_axis=1, tiled=True)  8.63 us
  transfers between devices with their start and end apart: 8, of which 4 were waited for; matrix products, arithmetic and copies ran while one was open for 28% of the time, Pallas kernels for 0%

profile of v1, /device:TPU:6, one launch (start us, length us, event | category | flops | bytes accessed | tf_op | source)
XLA Modules:
  0.0 365.0 jit_solution(6633827243841249071)
XLA Ops:
  7.2 0.0 all-gather.7.cloned.1.call-start
  7.2 7.0 %copy.119 = f32[16,64,1024]{1,2,0:T(8,128)} copy(f32[16,64,1024]{2,1,0:T(8,128)} %param.8) | data formatting | bytes 8388608 | tf_op args[0]
  14.3 3.2 copy.118
  17.5 7.6 %abs_reduce_fusion = f32[16,1024]{1,0:T(8,128)} fusion(f32[16,64,1024]{1,2,0:T(8,128)} %copy.119, bf16[16,64,1024]{1,2,0:T(8,128)(2,1)} %copy.118), kind=kLoop, calls=%fused_computation.1 | loop fusion | flops 4177920 | bytes 6356992 | tf_op jit(solution)/shard_map/reduce_max | solution.py:41
  25.1 0.0 all-gather.9.cloned.1.call-start
  25.2 3.6 abs_reduce_fusion.2
  28.8 0.0 all-gather.9.cloned.1.call-update
  28.8 0.8 reshape.43
  29.6 11.1 %all-to-all-start.3 = ((bf16[32,2,512]{2,1,0:T(2,128)(2,1)}), bf16[32,2,512]{2,1,0:T(2,128)(2,1)S(1)}, u32[]{:S(2)}, u32[]{:S(2)}) async-start(bf16[32,2,512]{2,1,0:T(2,128)(2,1)} %reshape.43), calls=%async_computation.3 | async-start | bytes 131072 | tf_op jit(solution)/shard_map/all_to_all | solution.py:20
  40.7 0.0 all-gather.11.cloned.1.call-start
  40.7 4.3 %abs_reduce_fusion.1 = f32[16,1024]{1,0:T(8,128)} fusion(f32[16,1024,64]{1,2,0:T(8,128)} %param.12, bf16[16,1024,64]{1,2,0:T(8,128)(2,1)} %param.13), kind=kLoop, calls=%fused_computation.4 | loop fusion | flops 4177920 | bytes 6356992 | tf_op jit(solution)/shard_map/reduce_max | solution.py:43
  45.0 3.0 all-to-all-done.3
  48.0 0.1 reshape.44
  48.2 0.2 reshape.32
  48.4 0.7 broadcast_in_dim.5
  49.1 4.2 %all-to-all-start.4 = ((bf16[4,2048,16]{1,2,0:T(8,128)(2,1)}), bf16[4,2048,16]{1,2,0:T(8,128)(2,1)S(1)}, u32[]{:S(2)}, u32[]{:S(2)}) async-start(bf16[4,2048,16]{1,2,0:T(8,128)(2,1)} %broadcast_in_dim.5), calls=%async_computation.4 | async-start | bytes 524288 | tf_op jit(solution)/shard_map/all_to_all | solution.py:20
  53.3 43.3 %all-gather.7.cloned.1.call-done = f32[512,1024]{1,0:T(8,128)} async-done(((f32[16,1024]{1,0:T(8,128)}), f32[512,1024]{1,0:T(8,128)}) %all-gather.7.cloned.1.call-update) | async-done | bytes 2097168 | tf_op jit(solution)/shard_map/all_gather | solution.py:8
  96.6 1.7 reduce_max.55
  98.3 6.1 %divide_convert_fusion = bf16[16,64,1024]{1,2,0:T(8,128)(2,1)S(1)} fusion(f32[16,64,1024]{1,2,0:T(8,128)} %copy.119, bf16[16,64,1024]{1,2,0:T(8,128)(2,1)} %copy.118, f32[16,1024]{1,0:T(8,128)S(1)} %reduce_max.55), kind=kLoop, calls=%fused_computation | loop fusion | flops 4194304 | bytes 8454144 | tf_op jit(solution)/shard_map/convert_element_type | solution.py:46
  105.3 1.9 copy-done.1
  107.3 7.9 %reshape.37 = bf16[32,2,16384]{2,1,0:T(2,128)(2,1)} reshape(bf16[32,16,32,64]{3,2,1,0:T(8,128)(2,1)} %bitcast.168) | data formatting | bytes 4194304
  115.1 8.6 %all-to-all-start = ((bf16[32,2,16384]{2,1,0:T(2,128)(2,1)}), bf16[32,2,16384]{2,1,0:T(2,128)(2,1)S(1)}, u32[]{:S(2)}, u32[]{:S(2)}) async-start(bf16[32,2,16384]{2,1,0:T(2,128)(2,1)} %reshape.37), calls=%async_computation | async-start | bytes 4194304 | tf_op jit(solution)/shard_map/all_to_all | solution.py:52
  123.7 56.0 %all-gather.9.cloned.1.call-done = f32[512,1024]{1,0:T(8,128)} async-done(((f32[16,1024]{1,0:T(8,128)}), f32[512,1024]{1,0:T(8,128)}) %all-gather.9.cloned.1.call-update) | async-done | bytes 2097168 | tf_op jit(solution)/shard_map/all_gather | solution.py:8
  179.7 1.7 reduce_max.57
  181.4 5.0 %divide_convert_fusion.2 = bf16[16,64,1024]{2,1,0:T(8,128)(2,1)} fusion(f32[16,64,1024]{2,1,0:T(8,128)} %param.10, bf16[16,64,1024]{2,1,0:T(8,128)(2,1)} %param.11, f32[16,1024]{1,0:T(8,128)S(1)} %reduce_max.57), kind=kLoop, calls=%fused_computation.6 | loop fusion | flops 4194304 | bytes 8454144 | tf_op jit(solution)/shard_map/convert_element_type | solution.py:47
  186.4 6.2 %copy.123 = bf16[16,64,1024]{1,0,2:T(8,128)(2,1)} copy(bf16[16,64,1024]{2,1,0:T(8,128)(2,1)} %divide_convert_fusion.2) | data formatting | bytes 4194304 | tf_op jit(solution)/shard_map/convert_element_type | solution.py:47
  192.6 7.9 %reshape.39 = bf16[32,2,16384]{2,1,0:T(2,128)(2,1)} reshape(bf16[1024,16,64]{2,1,0:T(8,128)(2,1)} %bitcast.164) | data formatting | bytes 4194304
  200.5 8.6 %all-to-all-start.1 = ((bf16[32,2,16384]{2,1,0:T(2,128)(2,1)}), bf16[32,2,16384]{2,1,0:T(2,128)(2,1)}, u32[]{:S(2)}, u32[]{:S(2)}) async-start(bf16[32,2,16384]{2,1,0:T(2,128)(2,1)} %reshape.39), calls=%async_computation.1 | async-start | bytes 4194304 | tf_op jit(solution)/shard_map/all_to_all | solution.py:57
  209.1 55.8 %all-gather.11.cloned.1.call-done = f32[512,1024]{1,0:T(8,128)} async-done(((f32[16,1024]{1,0:T(8,128)}), f32[512,1024]{1,0:T(8,128)}) %all-gather.11.cloned.1.call-update) | async-done | bytes 2097168 | tf_op jit(solution)/shard_map/all_gather | solution.py:8
  264.9 1.7 reduce_max.59
  266.6 5.0 %divide_convert_fusion.1 = bf16[16,1024,64]{1,2,0:T(8,128)(2,1)} fusion(f32[16,1024,64]{1,2,0:T(8,128)} %param.12, bf16[16,1024,64]{1,2,0:T(8,128)(2,1)} %param.13, f32[16,1024]{1,0:T(8,128)S(1)} %reduce_max.59), kind=kLoop, calls=%fused_computation.3 | loop fusion | flops 4194304 | bytes 8454144 | tf_op jit(solution)/shard_map/convert_element_type | solution.py:48
  271.6 6.2 %copy.128 = bf16[16,1024,64]{2,0,1:T(8,128)(2,1)} copy(bf16[16,1024,64]{1,2,0:T(8,128)(2,1)} %divide_convert_fusion.1) | data formatting | bytes 4194304 | tf_op jit(solution)/shard_map/convert_element_type | solution.py:48
  277.8 7.9 %reshape.41 = bf16[32,2,16384]{2,1,0:T(2,128)(2,1)} reshape(bf16[1024,16,64]{2,1,0:T(8,128)(2,1)} %bitcast.165) | data formatting | bytes 4194304
  285.6 8.6 %all-to-all-start.2 = ((bf16[32,2,16384]{2,1,0:T(2,128)(2,1)}), bf16[32,2,16384]{2,1,0:T(2,128)(2,1)}, u32[]{:S(2)}, u32[]{:S(2)}) async-start(bf16[32,2,16384]{2,1,0:T(2,128)(2,1)} %reshape.41), calls=%async_computation.2 | async-start | bytes 4194304 | tf_op jit(solution)/shard_map/all_to_all | solution.py:59
  294.3 0.7 constant_dynamic-slice_fusion.2
  295.0 0.7 constant_dynamic-slice_fusion
  295.7 0.7 constant_dynamic-slice_fusion.1
  296.3 4.0 %reshape.38 = bf16[32,16,32,64]{3,2,1,0:T(8,128)(2,1)} reshape(bf16[32,2,16384]{2,1,0:T(2,128)(2,1)S(1)} %all-to-all-done) | data formatting | bytes 4194304
  300.3 3.0 bitcast_bitcast_fusion
  303.3 4.6 %copy.120 = bf16[16,32,64,32]{2,1,3,0:T(8,128)(2,1)} copy(bf16[16,32,64,32]{2,3,0,1:T(8,128)(2,1)S(1)} %bitcast_bitcast_fusion) | data formatting | bytes 4194304 | tf_op jit(solution)/shard_map/reshape | solution.py:51
  308.0 6.7 %reshape.31 = bf16[16,2048,32]{1,2,0:T(8,128)(2,1)} reshape(bf16[16,32,64,32]{2,1,3,0:T(8,128)(2,1)} %copy.120) | data formatting | bytes 4194304 | tf_op jit(solution)/shard_map/reshape | solution.py:51
  314.7 7.9 %reshape.40 = bf16[1024,16,64]{2,1,0:T(8,128)(2,1)} reshape(bf16[32,2,16384]{2,1,0:T(2,128)(2,1)} %all-to-all-done.1) | data formatting | bytes 4194304
  322.6 6.9 %copy.125 = bf16[16,32,64,32]{2,1,3,0:T(8,128)(2,1)} copy(bf16[16,32,64,32]{2,0,3,1:T(8,128)(2,1)} %bitcast.166) | data formatting | bytes 4194304 | tf_op jit(solution)/shard_map/all_to_all | solution.py:57
  329.5 6.7 %all_to_all.39 = bf16[16,2048,32]{1,2,0:T(8,128)(2,1)} reshape(bf16[16,32,64,32]{2,1,3,0:T(8,128)(2,1)} %copy.125) | data formatting | bytes 4194304 | tf_op jit(solution)/shard_map/all_to_all | solution.py:57
  336.2 7.9 %reshape.42 = bf16[1024,16,64]{2,1,0:T(8,128)(2,1)} reshape(bf16[32,2,16384]{2,1,0:T(2,128)(2,1)} %all-to-all-done.2) | data formatting | bytes 4194304
  344.2 6.9 %copy.130 = bf16[16,32,32,64]{3,2,1,0:T(8,128)(2,1)} copy(bf16[16,32,32,64]{3,0,1,2:T(8,128)(2,1)} %bitcast.167) | data formatting | bytes 4194304 | tf_op jit(solution)/shard_map/all_to_all | solution.py:59
  351.0 6.7 %all_to_all.43 = bf16[16,32,2048]{2,1,0:T(8,128)(2,1)} reshape(bf16[16,32,32,64]{3,2,1,0:T(8,128)(2,1)} %copy.130) | data formatting | bytes 4194304 | tf_op jit(solution)/shard_map/all_to_all | solution.py:59
  357.8 0.7 copy.168
  (50 shorter events, 0.8 us)
Async XLA Ops:
  7.2 7.1 %copy-start.2 = (bf16[16,64,1024]{2,1,0:T(8,128)(2,1)S(1)}, bf16[16,64,1024]{2,1,0:T(8,128)(2,1)}, u32[]{:S(2)}) copy-start(bf16[16,64,1024]{2,1,0:T(8,128)(2,1)} %param.9) | copy-start | bytes 6291460
  7.2 89.4 %all-gather.7.cloned.1.call-start = ((), (), s32[]{:S(2)}) async-start(), calls=%async_computation.5 | async-start | bytes 2162688 | tf_op jit(solution)/shard_map/all_gather | solution.py:8
  17.5 7.7 %copy-start = (bf16[16,64,1024]{2,1,0:T(8,128)(2,1)S(1)}, bf16[16,64,1024]{2,1,0:T(8,128)(2,1)}, u32[]{:S(2)}) copy-start(bf16[16,64,1024]{2,1,0:T(8,128)(2,1)} %param.11) | copy-start | bytes 6291460
  25.1 3.7 %copy-start.3 = (f32[64,16]{0,1:T(8,128)S(1)}, f32[64,16]{0,1:T(8,128)}, u32[]{:S(2)}) copy-start(f32[64,16]{0,1:T(8,128)} %param.14) | copy-start | bytes 12292
  25.1 3.7 %copy-start.4 = (f32[64]{0:T(128)S(1)}, f32[64]{0:T(128)}, u32[]{:S(2)}) copy-start(f32[64]{0:T(128)} %param.15) | copy-start | bytes 772
  25.1 154.6 %all-gather.9.cloned.1.call-start = ((), (), s32[]{:S(2)}) async-start(), calls=%async_computation.6 | async-start | bytes 2162688 | tf_op jit(solution)/shard_map/all_gather | solution.py:8
  29.6 18.4 %all-to-all-start.3 = ((bf16[32,2,512]{2,1,0:T(2,128)(2,1)}), bf16[32,2,512]{2,1,0:T(2,128)(2,1)S(1)}, u32[]{:S(2)}, u32[]{:S(2)}) async-start(bf16[32,2,512]{2,1,0:T(2,128)(2,1)} %reshape.43), calls=%async_computation.3 | async-start | bytes 131072 | tf_op jit(solution)/shard_map/all_to_all | solution.py:20
  40.7 224.2 %all-gather.11.cloned.1.call-start = ((), (), s32[]{:S(2)}) async-start(), calls=%async_computation.7 | async-start | bytes 2162688 | tf_op jit(solution)/shard_map/all_gather | solution.py:8
  49.1 66.0 %all-to-all-start.4 = ((bf16[4,2048,16]{1,2,0:T(8,128)(2,1)}), bf16[4,2048,16]{1,2,0:T(8,128)(2,1)S(1)}, u32[]{:S(2)}, u32[]{:S(2)}) async-start(bf16[4,2048,16]{1,2,0:T(8,128)(2,1)} %broadcast_in_dim.5), calls=%async_computation.4 | async-start | bytes 524288 | tf_op jit(solution)/shard_map/all_to_all | solution.py:20
  105.3 1.9 copy-start.1
  115.1 85.3 %all-to-all-start = ((bf16[32,2,16384]{2,1,0:T(2,128)(2,1)}), bf16[32,2,16384]{2,1,0:T(2,128)(2,1)S(1)}, u32[]{:S(2)}, u32[]{:S(2)}) async-start(bf16[32,2,16384]{2,1,0:T(2,128)(2,1)} %reshape.37), calls=%async_computation | async-start | bytes 4194304 | tf_op jit(solution)/shard_map/all_to_all | solution.py:52
  200.5 85.2 %all-to-all-start.1 = ((bf16[32,2,16384]{2,1,0:T(2,128)(2,1)}), bf16[32,2,16384]{2,1,0:T(2,128)(2,1)}, u32[]{:S(2)}, u32[]{:S(2)}) async-start(bf16[32,2,16384]{2,1,0:T(2,128)(2,1)} %reshape.39), calls=%async_computation.1 | async-start | bytes 4194304 | tf_op jit(solution)/shard_map/all_to_all | solution.py:57
  285.6 50.6 %all-to-all-start.2 = ((bf16[32,2,16384]{2,1,0:T(2,128)(2,1)}), bf16[32,2,16384]{2,1,0:T(2,128)(2,1)}, u32[]{:S(2)}, u32[]{:S(2)}) async-start(bf16[32,2,16384]{2,1,0:T(2,128)(2,1)} %reshape.41), calls=%async_computation.2 | async-start | bytes 4194304 | tf_op jit(solution)/shard_map/all_to_all | solution.py:59
Sparse Core Ops, SparseCore 0:
  25.2 71.2 all-gather.6
  100.2 79.4 all-gather.8
  183.4 81.4 all-gather.10
